TPU v7x, 256 devices: a 4x2x16 block of a 4x16x16 slice. The times are simulated.
256 devices in a mesh: parts: 2 (over y), dp: 64 (over x, z), tensor: 2 (over core).
Axes of the slice: x: 4, y: 2, z: 16, core: 2. Of those that a mesh axis runs over, the one named last changes fastest.
The devices are a block of a 4x16x16 slice.
Arguments:
- normed: bfloat16 [128, 256, 4096], P(('parts', 'dp')), parts along dimension 0, may hold values from -28 to 28
- q_weight: bfloat16 [4096, 2048], P('dp', 'tensor'), may hold values from -0.09375 to 0.09375
- kv_weight: bfloat16 [4096, 2, 512], P('dp', None, 'tensor'), may hold values from -0.09375 to 0.09375
- o_weight: bfloat16 [2048, 4096], P('tensor', 'dp'), may hold values from -0.5 to 0.5
- lengths: int32 [128], P(('parts', 'dp')), parts along dimension 0, may hold values from 64 to 256
- destinations: int32 [128], P(('parts', 'dp')), parts along dimension 0, may hold values from 0 to 63, each once
Outputs:
- projected: bfloat16 [128, 256, 4096], P(('parts', 'dp'), None, 'tensor'), parts along dimension 0
- kv_cache: bfloat16 [128, 2, 4, 256, 128], P(('parts', 'dp'), None, None, 'tensor'), parts along dimension 0
There are 2 independent parts, one for each index of `parts`. A program takes and returns all parts, laid end to end along the dimension named above; an argument that names none is the same for every part. Nothing has to cross between parts.
All inputs are finite; a program needn't handle non-finite values.
Results may differ from a plain program's by a relative error of at most 0.012.
The roundings to bfloat16 on the way count: a program that leaves them out, or rounds other values in their place, can miss the bound.
Values may be sent and summed in bfloat16 or wider, within the bound.
No kernel may reach another device: no remote copies, remote signals or barrier semaphores. Data moves between devices by JAX's collectives and lax.ppermute only.
A program may use at most 128 MiB of HBM per device.

v0:
```python
import math
import jax
import jax.numpy as jnp
from jax import lax
from jax.sharding import PartitionSpec as P

HD = 128
ROPE_BASE = 500000.0


def copy_for_each(array, axis):
    copies = jnp.broadcast_to(array, (lax.axis_size(axis), *array.shape))
    return lax.all_to_all(copies, axis, split_axis=0, concat_axis=0, tiled=True)


def in_order(blocks, dim):
    blocks = jnp.moveaxis(blocks, 0, dim)
    lengths = blocks.shape
    return blocks.reshape(*lengths[:dim], lengths[dim] * lengths[dim + 1], *lengths[dim + 2 :])


def gather_directly(array, axis, dim):
    blocks = copy_for_each(array, axis)
    return in_order(blocks, dim)


def in_one_piece(arrays, axis, dim, along):
    widths = [math.prod(a.shape[along:]) for a in arrays]
    both = jnp.concatenate(
        [a.reshape(*a.shape[:along], w) for a, w in zip(arrays, widths)], axis=along
    )
    filled = lax.all_gather(both, axis, axis=dim, tiled=True)
    blocks = jnp.split(filled, [sum(widths[:k]) for k in range(1, len(widths))], axis=along)
    return tuple(
        (b.reshape(*filled.shape[:along], *a.shape[along:]) for a, b in zip(arrays, blocks))
    )


def in_blocks(array, dim, size):
    before, after = (array.shape[:dim], array.shape[dim + 1 :])
    return jnp.moveaxis(array.reshape(*before, size, -1, *after), dim, 0)


def summed_on_arrival(array, axis, dim):
    size = lax.axis_size(axis)
    blocks = lax.all_to_all(in_blocks(array, dim, size), axis, 0, 0, tiled=True)
    return jnp.sum(blocks, axis=0)


def rotate(values, positions):
    half = values.shape[-1] // 2
    steps = jnp.arange(half, dtype=jnp.float32) * (2.0 / values.shape[-1])
    freq = jnp.power(jnp.float32(ROPE_BASE), -steps)
    angle = positions.astype(jnp.float32)[:, None] * freq[None, :]
    cosine = jnp.cos(angle)[:, None, :]
    sine = jnp.sin(angle)[:, None, :]
    first = values[..., :half]
    second = values[..., half:]
    return jnp.concatenate(
        [first * cosine - second * sine, second * cosine + first * sine], axis=-1
    )


def attend(queries, keys, values, length):
    total = keys.shape[1]
    block = min(total, 512)
    count = total // block
    key_pos = jnp.arange(total, dtype=jnp.int32)

    def one_block(index):
        start = index * block
        scores = jnp.einsum(
            "kgqd,ktd->kgqt", queries, keys, preferred_element_type=jnp.float32
        ) / math.sqrt(HD)
        query_pos = start + jnp.arange(block, dtype=jnp.int32)
        allowed = (query_pos[:, None] >= key_pos[None, :]) & (key_pos[None, :] < length)
        scores = jnp.where(allowed, scores, -jnp.inf)
        peak = jnp.max(scores, axis=-1, keepdims=True)
        expo = jnp.exp(scores - peak)
        weights = (expo / jnp.sum(expo, axis=-1, keepdims=True)).astype(jnp.bfloat16)
        return jnp.einsum(
            "kgqt,ktd->kgqd", weights, values, preferred_element_type=jnp.float32
        ).astype(jnp.bfloat16)

    blocks = lax.map(one_block, jnp.arange(count, dtype=jnp.int32))
    return blocks.transpose(0, 3, 1, 2, 4).reshape(total, -1)


def regroup(cache):
    return lax.all_to_all(cache, "tensor", split_axis=2, concat_axis=1, tiled=True)


def deliver(cache, destination):
    count = lax.axis_size("dp")
    flat = cache.reshape(count, -1)
    sent_to = gather_directly(destination, "dp", 0)
    spread = lax.all_to_all(flat, "dp", split_axis=0, concat_axis=0, tiled=True)
    slots = jnp.arange(count, dtype=jnp.int32)
    match = sent_to[None, :] == slots[:, None]
    source = jnp.sum(jnp.where(match, slots[None, :], 0), axis=1)
    outgoing = jnp.take(spread, source, axis=0)
    arrived = lax.all_to_all(outgoing, "dp", split_axis=0, concat_axis=0, tiled=True)
    return arrived.reshape(cache.shape)


def on_device(normed, q_weight, kv_weight, o_weight, lengths, destinations):
    tokens = normed[0]
    total = tokens.shape[0]
    q_local = q_weight.shape[1] // HD
    kv_local = kv_weight.shape[2] // HD
    group = q_local // kv_local
    q_full, kv_full = in_one_piece((q_weight, kv_weight), "dp", 0, 1)
    query_raw = jnp.dot(tokens, q_full, preferred_element_type=jnp.float32)
    pair_raw = jnp.dot(
        tokens, kv_full.reshape(kv_full.shape[0], -1), preferred_element_type=jnp.float32
    )
    positions = jnp.arange(total, dtype=jnp.int32)
    query = rotate(query_raw.reshape(total, q_local, HD), positions).astype(jnp.bfloat16)
    pair = pair_raw.reshape(total, 2, kv_local, HD)
    keys = rotate(pair[:, 0], positions).astype(jnp.bfloat16)
    values = pair[:, 1].astype(jnp.bfloat16)
    grouped = query.reshape(total, kv_local, group, HD).transpose(1, 2, 0, 3)
    key_rows = keys.transpose(1, 0, 2)
    value_rows = values.transpose(1, 0, 2)
    length = lengths[0]
    attended = attend(grouped, key_rows, value_rows, length)
    partial_sums = jnp.dot(
        attended,
        lax.all_gather(o_weight, "dp", axis=1, tiled=True),
        preferred_element_type=jnp.float32,
    )
    projected = summed_on_arrival(partial_sums, "tensor", 1).astype(jnp.bfloat16)
    live = (positions < length)[None, :, None]
    kept_keys = jnp.where(live, key_rows, jnp.zeros_like(key_rows))
    kept_values = jnp.where(live, value_rows, jnp.zeros_like(value_rows))
    cache = jnp.stack([kept_keys, kept_values], axis=0)
    routed = deliver(regroup(cache), destinations)
    return (projected[None], routed[None])


def solution(mesh):
    placed = (
        P(("parts", "dp"), None, None),
        P("dp", "tensor"),
        P("dp", None, "tensor"),
        P("tensor", "dp"),
        P(("parts", "dp")),
        P(("parts", "dp")),
    )
    return jax.shard_map(
        on_device,
        mesh=mesh,
        in_specs=placed,
        out_specs=(
            P(("parts", "dp"), None, "tensor"),
            P(("parts", "dp"), None, None, "tensor", None),
        ),
        check_vma=False,
    )
```

profile of v0, /device:TPU:38, one launch (start us, length us, event | category | flops | bytes accessed | tf_op | source)
XLA Modules:
  0.0 402.5 jit_solution(113619744113657147)
XLA Ops:
  7.2 0.0 copy-start
  7.2 0.1 all-gather.3.cloned.1.call-start
  7.3 1.0 copy.79
  8.2 1.6 pad_maximum_fusion.1
  9.8 0.1 all-gather.3.cloned.1.call-update
  9.9 0.1 all-gather.5.cloned.1.call-start
  10.0 0.7 all-gather.5.cloned.1.call-update
  11.4 0.6 broadcast_in_dim.76
  12.0 28.4 %all-to-all-start.1 = ((s32[64,1,1]{2,1,0:T(1,128)}), s32[64,1,1]{2,1,0:T(1,128)S(1)}, u32[]{:S(2)}, u32[]{:S(2)}) async-start(s32[64,1,1]{2,1,0:T(1,128)} %broadcast_in_dim.76), calls=%async_computation.1 | async-start | bytes 65536 | tf_op jit(solution)/shard_map/all_to_all | solution.py:13
  41.1 0.3 multiply_cosine_fusion
  41.4 0.7 fusion.14
  42.1 0.7 copy.60
  42.8 0.7 copy.59
  43.6 8.7 %all-to-all-done.1 = s32[64,1,1]{2,1,0:T(1,128)S(1)} async-done(((s32[64,1,1]{2,1,0:T(1,128)}), s32[64,1,1]{2,1,0:T(1,128)S(1)}, u32[]{:S(2)}, u32[]{:S(2)}) %all-to-all-start.1) | async-done | bytes 288 | tf_op jit(solution)/shard_map/all_to_all | solution.py:13
  52.2 1.2 reduce
  53.5 0.1 select_reduce_fusion
  53.6 135.9 %all-gather.3.cloned.1.call-done = bf16[4096,1536]{1,0:T(8,128)(2,1)} async-done(((bf16[64,1536]{1,0:T(8,128)(2,1)}), bf16[4096,1536]{1,0:T(8,128)(2,1)}) %all-gather.3.cloned.1.call-update) | async-done | bytes 12582928 | tf_op jit(solution)/shard_map/all_gather | solution.py:32
  189.5 0.0 copy-done
  189.5 3.5 fusion.3
  193.0 5.8 %fusion.1 = f32[1024,256]{1,0:T(8,128)S(1)} fusion(bf16[4096,1536]{1,0:T(8,128)(2,1)} %all-gather.3.cloned.1.call-done, bf16[1,256,4096]{2,1,0:T(8,128)(2,1)S(1)} %copy-done), kind=kOutput, calls=%fused_computation.2 | convolution fusion | flops 2147483648 | bytes 11534336 | tf_op jit(solution)/shard_map/dot_general | solution.py:113
  198.8 0.2 subtract_convert_fusion
  199.0 0.3 copy.57
  199.3 1.0 copy.56
  200.3 0.1 copy.77
  200.4 0.1 copy.78
  200.5 0.0 copy-start.1
  200.5 1.2 subtract_convert_fusion.1
  201.7 0.0 copy-start.3
  201.7 0.1 fusion.22
  201.9 0.0 copy-done.1
  201.9 0.3 copy.65
  202.2 4.0 all_to_all.45
  206.2 0.0 copy-done.3
  206.2 0.1 all_to_all.39
  206.3 0.5 broadcast.133
  206.9 2.1 reduce.2
  209.0 0.9 reshape.172
  209.9 12.5 %all-to-all-start.3 = ((bf16[64,2,1024]{2,1,0:T(2,128)(2,1)}), bf16[64,2,1024]{2,1,0:T(2,128)(2,1)S(1)}, u32[]{:S(2)}, u32[]{:S(2)}) async-start(bf16[64,2,1024]{2,1,0:T(2,128)(2,1)} %reshape.172), calls=%async_computation.3 | async-start | bytes 524288 | tf_op jit(solution)/shard_map/all_to_all | solution.py:97
  222.4 0.0 copy-start.2
  222.4 3.5 fusion.30
  225.9 0.0 copy-done.2
  225.9 1.9 convolution_convert_fusion
  227.8 114.4 %all-gather.5.cloned.1.call-done = bf16[1024,4096]{0,1:T(8,128)(2,1)} async-done(((bf16[1024,64]{0,1:T(8,128)(2,1)}), bf16[1024,4096]{0,1:T(8,128)(2,1)}) %all-gather.5.cloned.1.call-update) | async-done | bytes 8388624 | tf_op jit(solution)/shard_map/all_gather | solution.py:129
  342.3 7.7 %convolution_bitcast_fusion = f32[2,256,2048]{2,1,0:T(8,128)} fusion(bf16[256,1024,1]{0,1,2:T(8,128)(2,1)S(1)} %bitcast.109, bf16[2,2048,1024]{2,1,0:T(8,128)(2,1)} %bitcast.108), kind=kOutput, calls=%fused_computation.6 | convolution fusion | flops 2147483648 | bytes 13107200 | tf_op jit(solution)/shard_map/dot_general | solution.py:127
  350.0 0.0 all-to-all-done.3
  350.0 5.6 %all-to-all-start = ((f32[2,256,2048]{2,1,0:T(8,128)}), f32[2,256,2048]{2,1,0:T(8,128)}, u32[]{:S(2)}, u32[]{:S(2)}) async-start(f32[2,256,2048]{2,1,0:T(8,128)} %convolution_bitcast_fusion), calls=%async_computation | async-start | bytes 8388608 | tf_op jit(solution)/shard_map/all_to_all | solution.py:46
  355.6 0.2 reshape.173
  355.9 0.2 copy.82
  356.0 0.7 gather_fusion
  356.8 0.1 bitcast_select_fusion
  356.9 0.7 reduce.3
  357.6 0.9 reshape.174
  358.5 1.6 all-to-all-done
  360.1 12.5 %all-to-all-start.4 = ((bf16[64,2,1024]{2,1,0:T(2,128)(2,1)}), bf16[64,2,1024]{2,1,0:T(2,128)(2,1)S(1)}, u32[]{:S(2)}, u32[]{:S(2)}) async-start(bf16[64,2,1024]{2,1,0:T(2,128)(2,1)} %reshape.174), calls=%async_computation.4 | async-start | bytes 524288 | tf_op jit(solution)/shard_map/all_to_all | solution.py:102
  372.6 3.8 reduce_sum.31
  376.3 16.7 %all-to-all-done.4 = bf16[64,2,1024]{2,1,0:T(2,128)(2,1)S(1)} async-done(((bf16[64,2,1024]{2,1,0:T(2,128)(2,1)}), bf16[64,2,1024]{2,1,0:T(2,128)(2,1)S(1)}, u32[]{:S(2)}, u32[]{:S(2)}) %all-to-all-start.4) | async-done | bytes 262176 | tf_op jit(solution)/shard_map/all_to_all | solution.py:102
  393.1 0.2 reshape.175
  393.3 1.5 reduce.1
  394.8 0.8 broadcast_in_dim_reshape.4
  (10 shorter events, 0.1 us)
Async XLA Ops:
  7.2 182.3 %copy-start = (bf16[1,256,4096]{2,1,0:T(8,128)(2,1)S(1)}, bf16[1,256,4096]{2,1,0:T(8,128)(2,1)}, u32[]{:S(2)}) copy-start(bf16[1,256,4096]{2,1,0:T(8,128)(2,1)} %param.6) | copy-start | bytes 6291460
  7.2 182.3 %all-gather.3.cloned.1.call-start = ((), (), s32[]{:S(2)}) async-start(), calls=%async_computation.5 | async-start | bytes 12779520 | tf_op jit(solution)/shard_map/all_gather | solution.py:32
  9.9 332.4 %all-gather.5.cloned.1.call-start = ((), (), s32[]{:S(2)}) async-start(), calls=%async_computation.6 | async-start | bytes 8519680 | tf_op jit(solution)/shard_map/all_gather | solution.py:129
  12.0 40.2 %all-to-all-start.1 = ((s32[64,1,1]{2,1,0:T(1,128)}), s32[64,1,1]{2,1,0:T(1,128)S(1)}, u32[]{:S(2)}, u32[]{:S(2)}) async-start(s32[64,1,1]{2,1,0:T(1,128)} %broadcast_in_dim.76), calls=%async_computation.1 | async-start | bytes 65536 | tf_op jit(solution)/shard_map/all_to_all | solution.py:13
  200.5 1.4 copy-start.1
  201.7 4.4 %copy-start.3 = (bf16[256,2,64]{2,0,1:T(8,128)(2,1)}, bf16[256,2,64]{2,0,1:T(8,128)(2,1)S(1)}, u32[]{:S(2)}) copy-start(bf16[256,2,64]{2,0,1:T(8,128)(2,1)S(1)} %get-tuple-element.19) | copy-start | bytes 196612
  209.9 140.1 %all-to-all-start.3 = ((bf16[64,2,1024]{2,1,0:T(2,128)(2,1)}), bf16[64,2,1024]{2,1,0:T(2,128)(2,1)S(1)}, u32[]{:S(2)}, u32[]{:S(2)}) async-start(bf16[64,2,1024]{2,1,0:T(2,128)(2,1)} %reshape.172), calls=%async_computation.3 | async-start | bytes 524288 | tf_op jit(solution)/shard_map/all_to_all | solution.py:97
  222.4 3.5 copy-start.2
  350.0 10.1 %all-to-all-start = ((f32[2,256,2048]{2,1,0:T(8,128)}), f32[2,256,2048]{2,1,0:T(8,128)}, u32[]{:S(2)}, u32[]{:S(2)}) async-start(f32[2,256,2048]{2,1,0:T(8,128)} %convolution_bitcast_fusion), calls=%async_computation | async-start | bytes 8388608 | tf_op jit(solution)/shard_map/all_to_all | solution.py:46
  360.1 33.0 %all-to-all-start.4 = ((bf16[64,2,1024]{2,1,0:T(2,128)(2,1)}), bf16[64,2,1024]{2,1,0:T(2,128)(2,1)S(1)}, u32[]{:S(2)}, u32[]{:S(2)}) async-start(bf16[64,2,1024]{2,1,0:T(2,128)(2,1)} %reshape.174), calls=%async_computation.4 | async-start | bytes 524288 | tf_op jit(solution)/shard_map/all_to_all | solution.py:102
Sparse Core Ops, SparseCore 0:
  11.0 178.4 all-gather.2
  191.9 150.3 all-gather.4
where the time goes:
time: 403 us; the launch traced here: 402 us
  waiting for transfers between devices  278 us (69%)
  starting transfers between devices  59.1 us (15%)
  matrix products  22.4 us (6%)
  between operations  15.6 us (4%)
  other arithmetic  13.7 us (3%)
  local copies, waits for them, and re-layouts  9.62 us (2%)
    all_gather x1, waiting for transfers between devices, in_one_piece(): filled = lax.all_gather(both, axis, axis=dim, tiled=True)  136 us
    all_gather x1, waiting for transfers between devices, on_device(): lax.all_gather(o_weight, 'dp', axis=1, tiled=True)  114 us
    all_to_all x1, starting transfers between devices, copy_for_each(): return lax.all_to_all(copies, axis, split_axis=0, concat_axis=0, tiled=True)  28.4 us
    all_to_all x1, waiting for transfers between devices, deliver(): lax.all_to_all(outgoing, 'dp', split_axis=0, concat_axis=0, tiled=True)  16.7 us
    all_to_all x1, starting transfers between devices, deliver(): lax.all_to_all(outgoing, 'dp', split_axis=0, concat_axis=0, tiled=True)  12.5 us
    all_to_all x1, starting transfers between devices, deliver(): spread = lax.all_to_all(flat, 'dp', split_axis=0, concat_axis=0, tiled=True)  12.5 us
    all_to_all x1, waiting for transfers between devices, copy_for_each(): return lax.all_to_all(copies, axis, split_axis=0, concat_axis=0, tiled=True)  8.67 us
  transfers between devices with their start and end apart: 6, of which 5 were waited for; matrix products, arithmetic and copies ran while one was open for 10% of the time, Pallas kernels for 0%

commit v1 on v0

--- a/solution.py
+++ b/solution.py
@@ -6,6 +6,13 @@
 
 HD = 128
 ROPE_BASE = 500000.0
+
+
+def all_by_exchange(block, name, dim):
+    size = lax.axis_size(name)
+    pieces = jnp.stack([block for _ in range(size)])
+    pieces = lax.all_to_all(pieces, name, split_axis=0, concat_axis=0)
+    return jnp.concatenate(pieces, axis=dim)
 
 
 def copy_for_each(array, axis):
@@ -125,9 +132,7 @@
     length = lengths[0]
     attended = attend(grouped, key_rows, value_rows, length)
     partial_sums = jnp.dot(
-        attended,
-        lax.all_gather(o_weight, "dp", axis=1, tiled=True),
-        preferred_element_type=jnp.float32,
+        attended, all_by_exchange(o_weight, "dp", 1), preferred_element_type=jnp.float32
     )
     projected = summed_on_arrival(partial_sums, "tensor", 1).astype(jnp.bfloat16)
     live = (positions < length)[None, :, None]

time: 403 us -> 684 us (1.70)
  waiting for transfers between devices: 278 us -> 551 us
  blocking collectives: 3.96 us -> 38.8 us
  starting transfers between devices: 59.1 us -> 28.5 us
    all_to_all x2 -> x1, waiting for transfers between devices: 18.3 us -> 346 us  [all_by_exchange(): pieces = lax.all_to_all(pieces, name, split_axis=0, concat_axis=0)]
    all_gather x1 -> x0, waiting for transfers between devices: 114 us -> none  [on_device(): lax.all_gather(o_weight, 'dp', axis=1, tiled=True)]
    all_gather x1, waiting for transfers between devices: 136 us -> 178 us  [in_one_piece(): filled = lax.all_gather(both, axis, axis=dim, tiled=True)]
    all_to_all x0 -> x2, blocking collectives: none -> 34.9 us  [the longest x1 26.7 us: deliver(): lax.all_to_all(outgoing, 'dp', split_axis=0, concat_axis=0, tiled=True)]
    all_to_all x1, waiting for transfers between devices: 0.01 us -> 18.6 us  [deliver(): spread = lax.all_to_all(flat, 'dp', split_axis=0, concat_axis=0, tiled=True)]
    all_to_all x1, starting transfers between devices: 28.4 us -> 12.5 us  [copy_for_each(): return lax.all_to_all(copies, axis, split_axis=0, concat_axis=0, tiled=True)]
    all_to_all x2 -> x1, starting transfers between devices: 18.1 us -> 7.9 us  [all_by_exchange(): pieces = lax.all_to_all(pieces, name, split_axis=0, concat_axis=0)]
  transfers between devices with their start and end apart: 6 -> 4, of which waited for: 5 -> 4; matrix products, arithmetic and copies ran while one was open for 10% -> 3% of each run, Pallas kernels for 0% -> 0%
where the time goes in v1:
time: 684 us; the launch traced here: 680 us
  waiting for transfers between devices  551 us (81%)
  blocking collectives  38.8 us (6%)
  starting transfers between devices  28.5 us (4%)
  matrix products  20.5 us (3%)
  between operations  15.7 us (2%)
  other arithmetic  12.7 us (2%)
  local copies, waits for them, and re-layouts  12.5 us (2%)
    all_to_all x1, waiting for transfers between devices, all_by_exchange(): pieces = lax.all_to_all(pieces, name, split_axis=0, concat_axis=0)  346 us
    all_gather x1, waiting for transfers between devices, in_one_piece(): filled = lax.all_gather(both, axis, axis=dim, tiled=True)  178 us
    all_to_all x1, blocking collectives, deliver(): lax.all_to_all(outgoing, 'dp', split_axis=0, concat_axis=0, tiled=True)  26.7 us
    all_to_all x1, waiting for transfers between devices, deliver(): spread = lax.all_to_all(flat, 'dp', split_axis=0, concat_axis=0, tiled=True)  18.6 us
  transfers between devices with their start and end apart: 4, of which 4 were waited for; matrix products, arithmetic and copies ran while one was open for 3% of the time, Pallas kernels for 0%

profile of v1, /device:TPU:38, one launch (start us, length us, event | category | flops | bytes accessed | tf_op | source)
XLA Modules:
  0.0 679.6 jit_solution(14051960783982347609)
XLA Ops:
  7.2 0.0 copy-start
  7.2 0.1 all-gather.2.cloned.1.call-start
  7.3 1.0 copy.79
  8.2 1.6 pad_maximum_fusion.1
  9.8 0.1 all-gather.2.cloned.1.call-update
  11.2 0.3 multiply_cosine_fusion
  11.5 0.1 copy.59
  11.6 0.1 copy.60
  11.8 177.7 %all-gather.2.cloned.1.call-done = bf16[4096,1536]{1,0:T(8,128)(2,1)} async-done(((bf16[64,1536]{1,0:T(8,128)(2,1)}), bf16[4096,1536]{1,0:T(8,128)(2,1)}) %all-gather.2.cloned.1.call-update) | async-done | bytes 12582928 | tf_op jit(solution)/shard_map/all_gather | solution.py:39
  189.5 0.0 copy-done
  189.5 3.5 fusion.3
  193.0 0.1 copy.78
  193.1 0.0 copy-start.1
  193.1 0.1 copy.77
  193.3 0.2 subtract_convert_fusion.1
  193.4 0.0 copy-start.3
  193.4 0.0 copy-start.4
  193.5 0.1 fusion.22
  193.6 0.5 copy-done.3
  194.1 0.1 copy-done.4
  194.2 0.3 copy.65
  194.5 4.0 all_to_all.50
  198.4 0.6 broadcast_in_dim.76
  199.1 12.5 %all-to-all-start.2 = ((s32[64,1,1]{2,1,0:T(1,128)}), s32[64,1,1]{2,1,0:T(1,128)S(1)}, u32[]{:S(2)}, u32[]{:S(2)}) async-start(s32[64,1,1]{2,1,0:T(1,128)} %broadcast_in_dim.76), calls=%async_computation.2 | async-start | bytes 65536 | tf_op jit(solution)/shard_map/all_to_all | solution.py:20
  211.5 0.0 copy-done.1
  211.6 0.1 all_to_all.43
  211.7 0.5 broadcast.135
  212.3 2.1 reduce.2
  214.4 0.9 reshape.182
  215.3 8.1 %all-to-all-done.2 = s32[64,1,1]{2,1,0:T(1,128)S(1)} async-done(((s32[64,1,1]{2,1,0:T(1,128)}), s32[64,1,1]{2,1,0:T(1,128)S(1)}, u32[]{:S(2)}, u32[]{:S(2)}) %all-to-all-start.2) | async-done | bytes 288 | tf_op jit(solution)/shard_map/all_to_all | solution.py:20
  223.4 8.1 %all-to-all-start.4 = ((bf16[64,2,1024]{2,1,0:T(2,128)(2,1)}), bf16[64,2,1024]{2,1,0:T(2,128)(2,1)S(1)}, u32[]{:S(2)}, u32[]{:S(2)}) async-start(bf16[64,2,1024]{2,1,0:T(2,128)(2,1)} %reshape.182), calls=%async_computation.4 | async-start | bytes 524288 | tf_op jit(solution)/shard_map/all_to_all | solution.py:104
  231.5 1.2 reduce
  232.7 0.1 select_reduce_fusion
  232.9 18.6 %all-to-all-done.4 = bf16[64,2,1024]{2,1,0:T(2,128)(2,1)S(1)} async-done(((bf16[64,2,1024]{2,1,0:T(2,128)(2,1)}), bf16[64,2,1024]{2,1,0:T(2,128)(2,1)S(1)}, u32[]{:S(2)}, u32[]{:S(2)}) %all-to-all-start.4) | async-done | bytes 262176 | tf_op jit(solution)/shard_map/all_to_all | solution.py:104
  251.4 0.2 reshape.183
  251.6 0.2 copy.82
  251.8 0.0 copy-start.5
  251.8 0.7 gather_fusion
  252.6 0.1 bitcast_select_fusion
  252.7 0.7 reduce.3
  253.4 0.2 reshape.184
  253.6 26.7 %all_to_all.51 = bf16[64,2,1024]{2,1,0:T(2,128)(2,1)S(1)} all-to-all(bf16[64,2,1024]{2,1,0:T(2,128)(2,1)S(1)} %reshape.184), channel_id=1, replica_groups=mesh['parts'=2,'dp'=64,'tensor'=2] {'dp'}, dimensions={0} | all-to-all | bytes 524288 | tf_op jit(solution)/shard_map/all_to_all | solution.py:109
  280.3 0.0 copy-done.5
  280.3 4.4 stack.8
  284.6 7.9 %all-to-all-start = ((bf16[64,1024,64]{1,2,0:T(8,128)(2,1)}), bf16[64,1024,64]{1,2,0:T(8,128)(2,1)}, u32[]{:S(2)}, u32[]{:S(2)}) async-start(bf16[64,1024,64]{1,2,0:T(8,128)(2,1)} %stack.8), calls=%async_computation | async-start | bytes 16777216 | tf_op jit(solution)/shard_map/all_to_all | solution.py:14
  292.5 0.7 fusion.14
  293.2 5.8 fusion.1
  299.0 0.2 subtract_convert_fusion
  299.2 0.3 copy.56
  299.5 1.0 copy.57
  300.5 0.0 copy-start.2
  300.5 3.5 fusion.30
  304.0 0.0 copy-done.2
  304.0 1.9 convolution_convert_fusion
  305.9 0.2 reshape.185
  306.2 1.5 reduce.1
  307.7 0.8 broadcast_in_dim_reshape.4
  308.5 346.5 %all-to-all-done = bf16[64,1024,64]{1,2,0:T(8,128)(2,1)} async-done(((bf16[64,1024,64]{1,2,0:T(8,128)(2,1)}), bf16[64,1024,64]{1,2,0:T(8,128)(2,1)}, u32[]{:S(2)}, u32[]{:S(2)}) %all-to-all-start) | async-done | bytes 8388640 | tf_op jit(solution)/shard_map/all_to_all | solution.py:14
  655.0 5.8 convolution_bitcast_fusion
  660.8 8.2 %all_to_all.52 = f32[2,256,2048]{2,1,0:T(8,128)} all-to-all(f32[2,256,2048]{2,1,0:T(8,128)S(1)} %convolution_bitcast_fusion), channel_id=1, replica_groups=mesh['parts'=2,'dp'=64,'tensor'=2] {'tensor'}, dimensions={0} | all-to-all | bytes 8388608 | tf_op jit(solution)/shard_map/all_to_all | solution.py:53
  669.0 3.8 reduce_sum.31
  (10 shorter events, 0.1 us)
Async XLA Ops:
  7.2 182.3 %copy-start = (bf16[1,256,4096]{2,1,0:T(8,128)(2,1)S(1)}, bf16[1,256,4096]{2,1,0:T(8,128)(2,1)}, u32[]{:S(2)}) copy-start(bf16[1,256,4096]{2,1,0:T(8,128)(2,1)} %param.6) | copy-start | bytes 6291460
  7.2 182.3 %all-gather.2.cloned.1.call-start = ((), (), s32[]{:S(2)}) async-start(), calls=%async_computation.6 | async-start | bytes 12779520 | tf_op jit(solution)/shard_map/all_gather | solution.py:39
  193.1 18.4 %copy-start.1 = (bf16[256,1,2,128]{3,0,2,1:T(8,128)(2,1)}, bf16[256,1,2,128]{3,0,2,1:T(8,128)(2,1)S(1)}, u32[]{:S(2)}) copy-start(bf16[256,1,2,128]{3,0,2,1:T(8,128)(2,1)S(1)} %copy.78) | copy-start | bytes 393220
  193.4 0.6 copy-start.3
  193.4 0.7 copy-start.4
  199.1 24.3 %all-to-all-start.2 = ((s32[64,1,1]{2,1,0:T(1,128)}), s32[64,1,1]{2,1,0:T(1,128)S(1)}, u32[]{:S(2)}, u32[]{:S(2)}) async-start(s32[64,1,1]{2,1,0:T(1,128)} %broadcast_in_dim.76), calls=%async_computation.2 | async-start | bytes 65536 | tf_op jit(solution)/shard_map/all_to_all | solution.py:20
  223.4 28.0 %all-to-all-start.4 = ((bf16[64,2,1024]{2,1,0:T(2,128)(2,1)}), bf16[64,2,1024]{2,1,0:T(2,128)(2,1)S(1)}, u32[]{:S(2)}, u32[]{:S(2)}) async-start(bf16[64,2,1024]{2,1,0:T(2,128)(2,1)} %reshape.182), calls=%async_computation.4 | async-start | bytes 524288 | tf_op jit(solution)/shard_map/all_to_all | solution.py:104
  251.8 28.4 %copy-start.5 = (bf16[1024,64]{0,1:T(8,128)(2,1)S(1)}, bf16[1024,64]{0,1:T(8,128)(2,1)}, u32[]{:S(2)}) copy-start(bf16[1024,64]{0,1:T(8,128)(2,1)} %param.9) | copy-start | bytes 393220
  284.6 370.4 %all-to-all-start = ((bf16[64,1024,64]{1,2,0:T(8,128)(2,1)}), bf16[64,1024,64]{1,2,0:T(8,128)(2,1)}, u32[]{:S(2)}, u32[]{:S(2)}) async-start(bf16[64,1024,64]{1,2,0:T(8,128)(2,1)} %stack.8), calls=%async_computation | async-start | bytes 16777216 | tf_op jit(solution)/shard_map/all_to_all | solution.py:14
  300.5 3.5 copy-start.2
Sparse Core Ops, SparseCore 0:
  11.0 178.4 all-gather.1
